TPU v7x, 32 devices: a whole 2x2x4 slice. The times are simulated.
32 devices in a mesh: heads: 4 (over y, x), seq: 8 (over z, core).
Axes of the slice: x: 2, y: 2, z: 4, core: 2. Of those that a mesh axis runs over, the one named last changes fastest.
Arguments:
- query: bfloat16 [24, 128, 576], P(None, 'heads'), may hold values from -1024 to 1024
- cache: bfloat16 [4096, 576], P('seq'), may hold values from -8 to 8
- segments: int32 [4096], P('seq'), may hold values from 0 to 3, as said below
- groups: int32 [24], replicated, may hold values from 0 to 3
- value_up: bfloat16 [128, 512, 128], P('heads'), may hold values from -3 to 3
- out_proj: bfloat16 [16384, 7168], P('heads', 'seq'), may hold values from -0.046875 to 0.046875
- targets: float32 [24, 7168], P(None, 'seq'), may hold values from -20 to 20
Outputs:
- projected: float32 [24, 7168], P(None, 'seq')
- loss: float32 [], replicated
- query_grad: float32 [24, 128, 576], P(None, 'heads')
- cache_grad: float32 [4096, 576], P('seq', 'heads')
Inputs may be any that keep to these rules, and one draw needn't show every extreme that they name: `segments`: constant over each aligned tile of 128 cached tokens; every group number appears in some tile.
All inputs are finite; a program needn't handle non-finite values.
Results may differ from a plain program's by a relative error of at most 0.015.
Values may be sent and summed in bfloat16 or wider, within the bound.
No kernel may reach another device: no remote copies, remote signals or barrier semaphores. Data moves between devices by JAX's collectives and lax.ppermute only.
A program may use at most 64 MiB of HBM per device.

v0:
```python
import jax
import jax.numpy as jnp
from jax import lax
from jax.sharding import PartitionSpec as P

scale_factor = 0.07216878364870322
floor_value = -1e30


def on_device(query, cache, segments, groups, value_up, out_proj, targets):
    query_len, head_count, width = query.shape
    latent = value_up.shape[1]
    vwidth = value_up.shape[2]
    row_count = query_len * head_count
    cache_len = cache.shape[0]
    query_rows = query.reshape(row_count, width)
    values = cache[:, :latent]
    allowed = groups[:, None] == segments[None, :]
    allowed_rows = jnp.broadcast_to(
        allowed[:, None, :], (query_len, head_count, cache_len)
    ).reshape(row_count, cache_len)
    scores = (
        jnp.einsum("rc,tc->rt", query_rows, cache, preferred_element_type=jnp.float32)
        * scale_factor
    )
    masked = jnp.where(allowed_rows, scores, floor_value)
    local_top = jnp.max(masked, axis=1)
    maximum = lax.pmax(local_top, "seq")
    weights = jnp.where(allowed_rows, jnp.exp(masked - maximum[:, None]), 0.0)
    totals = lax.psum(jnp.sum(weights, axis=1), "seq")
    partial_latent = jnp.dot(
        weights.astype(jnp.bfloat16), values, preferred_element_type=jnp.float32
    )
    portion = lax.psum_scatter(partial_latent, "seq", scatter_dimension=0, tiled=True)
    share_rows = portion.shape[0]
    start = lax.axis_index("seq") * share_rows
    share_totals = lax.dynamic_slice_in_dim(totals, start, share_rows)
    share_latent = (portion / share_totals[:, None]).astype(jnp.bfloat16)
    head_ids = (start + jnp.arange(share_rows, dtype=jnp.int32)) % head_count
    row_weights = jnp.take(value_up, head_ids, axis=0)
    share_value = jnp.einsum(
        "rc,rcv->rv", share_latent, row_weights, preferred_element_type=jnp.float32
    ).astype(jnp.bfloat16)
    value_out = lax.all_gather(share_value, "seq", axis=0, tiled=True).reshape(
        query_len, head_count, vwidth
    )
    flattened = value_out.reshape(query_len, head_count * vwidth)
    partial_proj = jnp.dot(flattened, out_proj, preferred_element_type=jnp.float32)
    projected = lax.psum(partial_proj, "heads")
    residual = projected - targets
    square_part = jnp.sum(residual * residual)
    model_width = targets.shape[1] * lax.axis_size("seq")
    d_projected = residual.astype(jnp.bfloat16)
    value_partial = jnp.einsum(
        "qd,rd->qr", d_projected, out_proj, preferred_element_type=jnp.float32
    )
    d_value = lax.psum(value_partial, "seq").reshape(query_len, head_count, vwidth)
    d_latent = (
        jnp.einsum(
            "qhv,hcv->qhc",
            d_value.astype(jnp.bfloat16),
            value_up,
            preferred_element_type=jnp.float32,
        )
        .astype(jnp.bfloat16)
        .reshape(row_count, latent)
    )
    row_dot = jnp.sum(d_value * value_out.astype(jnp.float32), axis=2).reshape(row_count)
    probs = weights / totals[:, None]
    d_probs = jnp.einsum("rc,tc->rt", d_latent, values, preferred_element_type=jnp.float32)
    d_scores = (scale_factor * probs * (d_probs - row_dot[:, None])).astype(jnp.bfloat16)
    query_part = jnp.dot(d_scores, cache, preferred_element_type=jnp.float32)
    square_total = lax.psum(square_part, "seq")
    query_sum = lax.psum(query_part, "seq")
    loss = square_total / (query_len * model_width)
    query_grad = query_sum.reshape(query_len, head_count, width)
    key_part = jnp.einsum("rt,rc->tc", d_scores, query_rows, preferred_element_type=jnp.float32)
    value_part = jnp.einsum(
        "rt,rc->tc", probs.astype(jnp.bfloat16), d_latent, preferred_element_type=jnp.float32
    )
    cache_part = key_part + jnp.concatenate(
        [value_part, jnp.zeros((cache_len, width - latent), jnp.float32)], axis=1
    )
    cache_grad = lax.psum_scatter(
        cache_part.astype(jnp.bfloat16), "heads", scatter_dimension=1, tiled=True
    ).astype(jnp.float32)
    return (projected, loss, query_grad, cache_grad)


def solution(mesh):
    in_specs = (
        P(None, "heads", None),
        P("seq", None),
        P("seq"),
        P(),
        P("heads", None, None),
        P("heads", "seq"),
        P(None, "seq"),
    )
    out_specs = (P(None, "seq"), P(), P(None, "heads", None), P("seq", "heads"))
    return jax.shard_map(
        on_device, mesh=mesh, in_specs=in_specs, out_specs=out_specs, check_vma=False
    )
```

profile of v0, /device:TPU:0, one launch (start us, length us, event | category | flops | bytes accessed | tf_op | source)
XLA Modules:
  0.0 309.5 jit_solution(6097966343069492329)
XLA Ops:
  7.2 0.0 reduce-scatter.3.cloned.1.call-start
  7.2 0.8 broadcast_compare_fusion
  8.1 0.1 broadcast_in_dim.29
  8.2 0.5 copy.29
  8.7 2.0 fusion.25
  10.7 18.1 %pmax.7 = f32[768]{0:T(1024)S(1)} all-reduce(f32[768]{0:T(1024)S(1)} %get-tuple-element.4), channel_id=1, replica_groups=mesh['heads'=4,'seq'=8] {'seq'}, use_global_device_ids=true, to_apply=%region_1.2 | all-reduce | flops 768 | bytes 6144 | tf_op jit(solution)/shard_map/pmax | solution.py:28
  28.8 1.8 fusion.8
  30.6 0.0 all-reduce.5.cloned.1.call-start
  30.7 0.4 fusion.15
  31.1 13.7 %psum.35 = f32[768]{0:T(1024)S(1)} all-reduce(f32[768]{0:T(1024)S(1)} %fusion.15), channel_id=1, replica_groups=mesh['heads'=4,'seq'=8] {'seq'}, use_global_device_ids=true, to_apply=%region_4.5 | all-reduce | flops 768 | bytes 6144 | tf_op jit(solution)/shard_map/psum | solution.py:30
  44.8 0.1 dynamic_slice.3
  44.9 0.5 copy-done.7
  45.4 8.8 %gather_fusion = bf16[96,512,128]{2,1,0:T(8,128)(2,1)} fusion(bf16[32,512,128]{2,1,0:T(8,128)(2,1)} %param.11, s32[1024]{0:T(1024)S(1)} %pad_clamp_fusion), kind=kCustom, calls=%fused_computation | custom fusion | bytes 25166208 | tf_op jit(solution)/shard_map/jit(_take)/gather | solution.py:40
  54.2 9.3 %reduce-scatter.3.cloned.1.call-done = f32[96,512]{1,0:T(8,128)} async-done(((f32[768,512]{1,0:T(8,128)}), f32[96,512]{1,0:T(8,128)}) %reduce-scatter.3.cloned.1.call-update) | async-done | bytes 196624 | tf_op jit(solution)/shard_map/reduce_scatter | solution.py:34
  63.5 1.0 fusion.16
  64.5 5.7 %fusion = f32[96,1,128]{2,1,0:T(1,128)S(1)} fusion(bf16[96,512,128]{2,1,0:T(8,128)(2,1)} %gather_fusion, pred[96]{0:T(512)(128)(4,1)S(1)} %compare_and_fusion, bf16[96,512,1]{1,0,2:T(8,128)(2,1)S(1)} %fusion.16), kind=kOutput, calls=%fused_computation.1 | convolution fusion | flops 18874368 | bytes 12730464 | tf_op jit(solution)/shard_map/rc,rcv->rv/dot_general | solution.py:41
  70.3 15.2 %all_gather.3 = bf16[768,128]{1,0:T(8,128)(2,1)} all-gather(bf16[96,128]{1,0:T(8,128)(2,1)S(1)} %convert_element_type.41), channel_id=1, replica_groups=mesh['heads'=4,'seq'=8] {'seq'}, dimensions={0}, use_global_device_ids=true | all-gather | bytes 221184 | tf_op jit(solution)/shard_map/all_gather | solution.py:44
  85.4 1.7 reshape_reshape.3
  87.1 4.9 %fusion.26 = f32[24,896]{1,0:T(8,128)} fusion(bf16[24,4096]{1,0:T(8,128)(2,1)} %reshape_reshape.3, bf16[4096,896]{1,0:T(8,128)(2,1)} %param.12), kind=kOutput, calls=%fused_computation.49 | convolution fusion | flops 176160768 | bytes 7622656 | tf_op jit(solution)/shard_map/dot_general | solution.py:48
  92.0 0.0 all-reduce.7.cloned.1.call-start
  92.1 39.5 %all-reduce.5.cloned.1.call-done = f32[24,896]{1,0:T(8,128)} async-done(((f32[24,896]{1,0:T(8,128)}), f32[24,896]{1,0:T(8,128)}) %all-reduce.5.cloned.1.call-update) | async-done | bytes 86032 | tf_op jit(solution)/shard_map/psum | solution.py:49
  131.6 5.5 %convolution_bitcast_fusion = f32[3,32,8,128]{3,2,1,0:T(8,128)S(1)} fusion(bf16[4096,896]{1,0:T(8,128)(2,1)} %param.12, f32[24,896]{1,0:T(8,128)} %all-reduce.5.cloned.1.call-done, f32[24,896]{1,0:T(8,128)} %param.13), kind=kOutput, calls=%fused_computation.12 | convolution fusion | flops 176203776 | bytes 7905280 | tf_op jit(solution)/shard_map/qd,rd->qr/dot_general | solution.py:54
  137.1 0.8 copy.47
  137.9 0.0 reduce-scatter.5.cloned.1.call-start
  138.0 1.7 convert.1
  139.7 54.9 %all-reduce.7.cloned.1.call-done = f32[24,32,128]{2,0,1:T(8,128)} async-done(((f32[24,32,128]{2,0,1:T(8,128)}), f32[24,32,128]{2,0,1:T(8,128)}) %all-reduce.7.cloned.1.call-update) | async-done | bytes 393232 | tf_op jit(solution)/shard_map/psum | solution.py:57
  194.6 1.4 fusion.12
  196.0 0.7 copy.33
  196.7 0.8 sub.24
  197.5 4.6 %fusion.5 = bf16[24,32,512]{2,0,1:T(8,128)(2,1)S(1)} fusion(bf16[32,512,128]{2,1,0:T(8,128)(2,1)} %param.11, f32[24,32,128]{2,0,1:T(8,128)} %all-reduce.7.cloned.1.call-done), kind=kOutput, calls=%fused_computation.11 | convolution fusion | flops 101154816 | bytes 5373952 | tf_op jit(solution)/shard_map/qhv,hcv->qhc/dot_general | solution.py:59
  202.1 0.0 copy-start.8
  202.1 0.2 copy.31
  202.3 0.4 copy-done.6
  202.8 0.8 fusion.6
  203.5 0.9 multiply_convert_fusion
  204.4 0.9 copy-done.1
  205.3 1.5 fusion.4
  206.8 0.0 all-reduce.9.cloned.1.call-start
  206.9 3.2 %fusion.27 = f32[768,576]{1,0:T(8,128)} fusion(bf16[768,512]{0,1:T(8,128)(2,1)} %copy-done.1, bf16[512,576]{0,1:T(8,128)(2,1)S(1)} %copy-done.2), kind=kOutput, calls=%fused_computation.50 | convolution fusion | flops 452984832 | bytes 3145728 | tf_op jit(solution)/shard_map/dot_general | solution.py:72
  210.1 0.9 copy-done.3
  211.0 0.0 copy-done.4
  211.0 0.6 multiply_reduce_fusion
  211.6 14.3 %psum.37 = f32[]{:T(128)} all-reduce(f32[]{:T(128)} %multiply_reduce_fusion), channel_id=1, replica_groups=mesh['heads'=4,'seq'=8] {'seq'}, use_global_device_ids=true, to_apply=%region_7.8 | all-reduce | flops 1 | bytes 8 | tf_op jit(solution)/shard_map/psum | solution.py:73
  226.6 4.8 %reduce-scatter.5.cloned.1.call-done = bf16[512,144]{0,1:T(8,128)(2,1)} async-done(((bf16[512,576]{0,1:T(8,128)(2,1)}), bf16[512,144]{0,1:T(8,128)(2,1)}) %reduce-scatter.5.cloned.1.call-update) | async-done | bytes 147472 | tf_op jit(solution)/shard_map/reduce_scatter | solution.py:84
  231.4 1.7 convert_element_type.51
  233.1 65.2 %all-reduce.9.cloned.1.call-done = f32[24,32,576]{2,1,0:T(8,128)} async-done(((f32[24,32,576]{2,1,0:T(8,128)}), f32[24,32,576]{2,1,0:T(8,128)}) %all-reduce.9.cloned.1.call-update) | async-done | bytes 1769488 | tf_op jit(solution)/shard_map/psum | solution.py:74
  298.3 0.6 copy.56
  298.9 2.9 copy.57
  (21 shorter events, 0.2 us)
Async XLA Ops:
  7.2 1.5 copy-start
  7.2 56.3 %reduce-scatter.3.cloned.1.call-start = ((), (), s32[]{:S(2)}) async-start(), calls=%async_computation.2 | async-start | bytes 1769472 | tf_op jit(solution)/shard_map/reduce_scatter | solution.py:34
  8.7 20.1 %copy-start.2 = (bf16[512,576]{0,1:T(8,128)(2,1)S(1)}, bf16[512,576]{0,1:T(8,128)(2,1)}, u32[]{:S(2)}) copy-start(bf16[512,576]{0,1:T(8,128)(2,1)} %param.8) | copy-start | bytes 1769476
  28.8 1.9 copy-start.5
  30.6 101.0 %all-reduce.5.cloned.1.call-start = ((), (), s32[]{:S(2)}) async-start(), calls=%async_computation.3 | async-start | bytes 172032 | tf_op jit(solution)/shard_map/psum | solution.py:49
  44.8 0.6 copy-start.7
  92.0 102.6 %all-reduce.7.cloned.1.call-start = ((), (), s32[]{:S(2)}) async-start(), calls=%async_computation.4 | async-start | bytes 786432 | tf_op jit(solution)/shard_map/psum | solution.py:57
  137.9 93.5 %reduce-scatter.5.cloned.1.call-start = ((), (), s32[]{:S(2)}) async-start(), calls=%async_computation.6 | async-start | bytes 737280 | tf_op jit(solution)/shard_map/reduce_scatter | solution.py:84
  202.1 0.7 copy-start.6
  202.1 0.7 copy-start.8
  204.4 0.9 copy-start.1
  206.8 91.4 %all-reduce.9.cloned.1.call-start = ((), (), s32[]{:S(2)}) async-start(), calls=%async_computation.5 | async-start | bytes 3932160 | tf_op jit(solution)/shard_map/psum | solution.py:74
  210.1 0.9 copy-start.3
  210.1 0.9 copy-start.4
Sparse Core Ops, SparseCore 0:
  30.8 32.6 reduce-scatter.2
  92.2 39.4 all-reduce.4
  138.0 56.5 all-reduce.6
  206.9 24.4 reduce-scatter.4
  234.2 63.9 all-reduce.8
where the time goes:
time: 310 us; the launch traced here: 309 us
  waiting for transfers between devices  174 us (56%)
  blocking collectives  61.3 us (20%)
  matrix products  30.8 us (10%)
  local copies, waits for them, and re-layouts  19.9 us (6%)
  between operations  15.7 us (5%)
  other arithmetic  7.67 us (2%)
    psum x1, waiting for transfers between devices, on_device(): query_sum = lax.psum(query_part, 'seq')  65.2 us
    psum x1, waiting for transfers between devices, on_device(): lax.psum(value_partial, 'seq').reshape(query_len, head_count, vwidth)  54.9 us
    psum x1, waiting for transfers between devices, on_device(): projected = lax.psum(partial_proj, 'heads')  39.5 us
    pmax x1, blocking collectives, on_device(): maximum = lax.pmax(local_top, 'seq')  18.1 us
    all_gather x1, blocking collectives, on_device(): lax.all_gather(share_value, 'seq', axis=0, tiled=True)  15.2 us
    psum x1, blocking collectives, on_device(): square_total = lax.psum(square_part, 'seq')  14.3 us
    psum x1, blocking collectives, on_device(): totals = lax.psum(jnp.sum(weights, axis=1), 'seq')  13.7 us
    reduce_scatter x1, waiting for transfers between devices, on_device(): lax.psum_scatter(partial_latent, 'seq', scatter_dimension=0, tiled=True)  9.28 us
  transfers between devices with their start and end apart: 5, of which 5 were waited for; matrix products, arithmetic and copies ran while one was open for 5% of the time, Pallas kernels for 0%

commit v1 on v0

--- a/solution.py
+++ b/solution.py
@@ -71,7 +71,8 @@
     d_scores = (scale_factor * probs * (d_probs - row_dot[:, None])).astype(jnp.bfloat16)
     query_part = jnp.dot(d_scores, cache, preferred_element_type=jnp.float32)
     square_total = lax.psum(square_part, "seq")
-    query_sum = lax.psum(query_part, "seq")
+    parts = lax.all_gather(query_part, "seq", axis=0, tiled=False)
+    query_sum = parts.sum(axis=0)
     loss = square_total / (query_len * model_width)
     query_grad = query_sum.reshape(query_len, head_count, width)
     key_part = jnp.einsum("rt,rc->tc", d_scores, query_rows, preferred_element_type=jnp.float32)

time: 310 us -> 400 us (1.29)
  waiting for transfers between devices: 174 us -> 239 us
  local copies, waits for them, and re-layouts: 19.9 us -> 34.6 us
  other arithmetic: 7.67 us -> 15 us
    all_gather x0 -> x1, waiting for transfers between devices: none -> 130 us  [on_device(): parts = lax.all_gather(query_part, 'seq', axis=0, tiled=False)]
    psum x1 -> x0, waiting for transfers between devices: 65.2 us -> none  [on_device(): query_sum = lax.psum(query_part, 'seq')]
    unnamed x20 -> x24, local copies, waits for them, and re-layouts: 6.34 us -> 19.2 us
    reduce_sum x0 -> x1, other arithmetic: none -> 8.39 us  [on_device(): query_sum = parts.sum(axis=0)]
  transfers between devices with their start and end apart: 5 -> 5, of which waited for: 5 -> 5; matrix products, arithmetic and copies ran while one was open for 5% -> 4% of each run, Pallas kernels for 0% -> 0%
where the time goes in v1:
time: 400 us; the launch traced here: 399 us
  waiting for transfers between devices  239 us (60%)
  blocking collectives  61.3 us (15%)
  local copies, waits for them, and re-layouts  34.6 us (9%)
  matrix products  32.8 us (8%)
  between operations  15.7 us (4%)
  other arithmetic  15 us (4%)
    all_gather x1, waiting for transfers between devices, on_device(): parts = lax.all_gather(query_part, 'seq', axis=0, tiled=False)  130 us
    psum x1, waiting for transfers between devices, on_device(): lax.psum(value_partial, 'seq').reshape(query_len, head_count, vwidth)  54.9 us
    psum x1, waiting for transfers between devices, on_device(): projected = lax.psum(partial_proj, 'heads')  39.6 us
    unnamed x24, local copies, waits for them, and re-layouts  19.2 us
    pmax x1, blocking collectives, on_device(): maximum = lax.pmax(local_top, 'seq')  18.1 us
    all_gather x1, blocking collectives, on_device(): lax.all_gather(share_value, 'seq', axis=0, tiled=True)  15.2 us
    psum x1, blocking collectives, on_device(): square_total = lax.psum(square_part, 'seq')  14.3 us
    psum x1, blocking collectives, on_device(): totals = lax.psum(jnp.sum(weights, axis=1), 'seq')  13.7 us
  transfers between devices with their start and end apart: 5, of which 5 were waited for; matrix products, arithmetic and copies ran while one was open for 4% of the time, Pallas kernels for 0%

profile of v1, /device:TPU:0, one launch (start us, length us, event | category | flops | bytes accessed | tf_op | source)
XLA Modules:
  0.0 399.0 jit_solution(9553835041896644769)
XLA Ops:
  7.2 0.0 reduce-scatter.3.cloned.1.call-start
  7.2 0.8 broadcast_compare_fusion
  8.1 0.1 broadcast_in_dim.29
  8.2 0.5 copy.27
  8.7 2.0 fusion.25
  10.7 18.1 %pmax.7 = f32[768]{0:T(1024)S(1)} all-reduce(f32[768]{0:T(1024)S(1)} %get-tuple-element.8), channel_id=1, replica_groups=mesh['heads'=4,'seq'=8] {'seq'}, use_global_device_ids=true, to_apply=%region_1.2 | all-reduce | flops 768 | bytes 6144 | tf_op jit(solution)/shard_map/pmax | solution.py:28
  28.8 1.8 fusion.8
  30.6 0.0 reduce-scatter.3.cloned.1.call-update
  30.6 0.0 all-reduce.4.cloned.1.call-start
  30.7 0.4 fusion.15
  31.1 13.7 %psum.28 = f32[768]{0:T(1024)S(1)} all-reduce(f32[768]{0:T(1024)S(1)} %fusion.15), channel_id=1, replica_groups=mesh['heads'=4,'seq'=8] {'seq'}, use_global_device_ids=true, to_apply=%region_4.5 | all-reduce | flops 768 | bytes 6144 | tf_op jit(solution)/shard_map/psum | solution.py:30
  44.8 0.1 dynamic_slice.3
  44.9 8.8 %gather_fusion = bf16[96,512,128]{2,1,0:T(8,128)(2,1)} fusion(bf16[32,512,128]{2,1,0:T(8,128)(2,1)} %param.11, s32[1024]{0:T(1024)S(1)} %pad_clamp_fusion), kind=kCustom, calls=%fused_computation | custom fusion | bytes 25166208 | tf_op jit(solution)/shard_map/jit(_take)/gather | solution.py:40
  53.7 9.7 %reduce-scatter.3.cloned.1.call-done = f32[96,512]{1,0:T(8,128)} async-done(((f32[768,512]{1,0:T(8,128)}), f32[96,512]{1,0:T(8,128)}) %reduce-scatter.3.cloned.1.call-update) | async-done | bytes 196624 | tf_op jit(solution)/shard_map/reduce_scatter | solution.py:34
  63.4 1.0 fusion.16
  64.4 5.8 %fusion = f32[96,1,128]{2,1,0:T(1,128)S(1)} fusion(bf16[96,512,128]{2,1,0:T(8,128)(2,1)} %gather_fusion, pred[96]{0:T(512)(128)(4,1)S(1)} %compare_and_fusion, bf16[96,512,1]{1,0,2:T(8,128)(2,1)S(1)} %fusion.16), kind=kOutput, calls=%fused_computation.2 | convolution fusion | flops 18874368 | bytes 12730464 | tf_op jit(solution)/shard_map/rc,rcv->rv/dot_general | solution.py:41
  70.2 15.2 %all_gather.9 = bf16[768,128]{1,0:T(8,128)(2,1)} all-gather(bf16[96,128]{1,0:T(8,128)(2,1)S(1)} %convert_element_type.41), channel_id=1, replica_groups=mesh['heads'=4,'seq'=8] {'seq'}, dimensions={0}, use_global_device_ids=true | all-gather | bytes 221184 | tf_op jit(solution)/shard_map/all_gather | solution.py:44
  85.3 1.7 reshape_reshape.3
  87.0 4.9 %fusion.26 = f32[24,896]{1,0:T(8,128)} fusion(bf16[24,4096]{1,0:T(8,128)(2,1)} %reshape_reshape.3, bf16[4096,896]{1,0:T(8,128)(2,1)} %param.12), kind=kOutput, calls=%fused_computation.50 | convolution fusion | flops 176160768 | bytes 7622656 | tf_op jit(solution)/shard_map/dot_general | solution.py:48
  92.0 0.0 all-reduce.6.cloned.1.call-start
  92.0 39.6 %all-reduce.4.cloned.1.call-done = f32[24,896]{1,0:T(8,128)} async-done(((f32[24,896]{1,0:T(8,128)}), f32[24,896]{1,0:T(8,128)}) %all-reduce.4.cloned.1.call-update) | async-done | bytes 86032 | tf_op jit(solution)/shard_map/psum | solution.py:49
  131.6 5.5 %convolution_bitcast_fusion = f32[3,32,8,128]{3,2,1,0:T(8,128)S(1)} fusion(bf16[4096,896]{1,0:T(8,128)(2,1)} %param.12, f32[24,896]{1,0:T(8,128)} %all-reduce.4.cloned.1.call-done, f32[24,896]{1,0:T(8,128)} %param.13), kind=kOutput, calls=%fused_computation.13 | convolution fusion | flops 176203776 | bytes 7905280 | tf_op jit(solution)/shard_map/qd,rd->qr/dot_general | solution.py:54
  137.1 0.8 copy.45
  137.9 0.0 reduce-scatter.5.cloned.1.call-start
  137.9 1.7 convert.1
  139.7 54.9 %all-reduce.6.cloned.1.call-done = f32[24,32,128]{2,0,1:T(8,128)} async-done(((f32[24,32,128]{2,0,1:T(8,128)}), f32[24,32,128]{2,0,1:T(8,128)}) %all-reduce.6.cloned.1.call-update) | async-done | bytes 393232 | tf_op jit(solution)/shard_map/psum | solution.py:57
  194.6 4.6 %fusion.5 = bf16[24,32,512]{2,0,1:T(8,128)(2,1)S(1)} fusion(bf16[32,512,128]{2,1,0:T(8,128)(2,1)} %param.11, f32[24,32,128]{2,0,1:T(8,128)} %all-reduce.6.cloned.1.call-done), kind=kOutput, calls=%fused_computation.12 | convolution fusion | flops 101154816 | bytes 5373952 | tf_op jit(solution)/shard_map/qhv,hcv->qhc/dot_general | solution.py:59
  199.2 0.3 copy.29
  199.5 1.7 fusion.6
  201.2 0.3 fusion.12
  201.5 0.7 copy.31
  202.2 0.8 sub.24
  203.0 2.1 multiply_convert_fusion
  205.1 0.9 copy-done.1
  206.0 1.5 fusion.4
  207.5 0.2 all-gather.3.cloned.1.call-start
  207.7 3.0 fusion.27
  210.7 0.9 copy-done.7
  211.6 0.0 copy-done.8
  211.6 0.6 multiply_reduce_fusion
  212.2 14.3 %psum.30 = f32[]{:T(128)} all-reduce(f32[]{:T(128)} %multiply_reduce_fusion), channel_id=1, replica_groups=mesh['heads'=4,'seq'=8] {'seq'}, use_global_device_ids=true, to_apply=%region_7.8 | all-reduce | flops 1 | bytes 8 | tf_op jit(solution)/shard_map/psum | solution.py:73
  227.2 4.9 %reduce-scatter.5.cloned.1.call-done = bf16[512,144]{0,1:T(8,128)(2,1)} async-done(((bf16[512,576]{0,1:T(8,128)(2,1)}), bf16[512,144]{0,1:T(8,128)(2,1)}) %reduce-scatter.5.cloned.1.call-update) | async-done | bytes 147472 | tf_op jit(solution)/shard_map/reduce_scatter | solution.py:85
  232.1 1.7 convert_element_type.51
  233.8 130.0 %all-gather.3.cloned.1.call-done = f32[6144,576]{0,1:T(8,128)} async-done(((f32[768,576]{0,1:T(8,128)}), f32[6144,576]{0,1:T(8,128)}) %all-gather.3.cloned.1.call-update) | async-done | bytes 14155792 | tf_op jit(solution)/shard_map/all_gather | solution.py:74
  363.8 16.8 %copy.38 = f32[72,8,8,768]{3,2,1,0:T(8,128)} copy(f32[72,8,8,768]{3,1,2,0:T(8,128)} %bitcast.38) | data formatting | bytes 28311552
  380.6 8.4 %bitcast_reduce_fusion = f32[768,576]{0,1:T(8,128)S(1)} fusion(f32[72,8,8,768]{3,2,1,0:T(8,128)} %copy.38), kind=kLoop, calls=%fused_computation.1 | loop fusion | flops 3096576 | bytes 15925248 | tf_op jit(solution)/shard_map/reduce_sum | solution.py:75
  389.0 1.8 copy.33
  390.7 0.6 copy.53
  (27 shorter events, 0.2 us)
Async XLA Ops:
  7.2 1.5 copy-start
  7.2 56.2 %reduce-scatter.3.cloned.1.call-start = ((), (), s32[]{:S(2)}) async-start(), calls=%async_computation.2 | async-start | bytes 1769472 | tf_op jit(solution)/shard_map/reduce_scatter | solution.py:34
  8.7 20.1 %copy-start.2 = (bf16[512,576]{0,1:T(8,128)(2,1)S(1)}, bf16[512,576]{0,1:T(8,128)(2,1)}, u32[]{:S(2)}) copy-start(bf16[512,576]{0,1:T(8,128)(2,1)} %param.8) | copy-start | bytes 1769476
  28.8 170.6 %copy-start.9 = (f32[768]{0:T(1024)}, f32[768]{0:T(1024)S(1)}, u32[]{:S(2)}) copy-start(f32[768]{0:T(1024)S(1)} %pmax.7) | copy-start | bytes 9220
  30.6 101.0 %all-reduce.4.cloned.1.call-start = ((), (), s32[]{:S(2)}) async-start(), calls=%async_computation.3 | async-start | bytes 172032 | tf_op jit(solution)/shard_map/psum | solution.py:49
  44.8 154.7 %copy-start.10 = (f32[768]{0:T(1024)}, f32[768]{0:T(1024)S(1)}, u32[]{:S(2)}) copy-start(f32[768]{0:T(1024)S(1)} %psum.28) | copy-start | bytes 9220
  92.0 102.6 %all-reduce.6.cloned.1.call-start = ((), (), s32[]{:S(2)}) async-start(), calls=%async_computation.4 | async-start | bytes 786432 | tf_op jit(solution)/shard_map/psum | solution.py:57
  137.9 94.2 %reduce-scatter.5.cloned.1.call-start = ((), (), s32[]{:S(2)}) async-start(), calls=%async_computation.5 | async-start | bytes 737280 | tf_op jit(solution)/shard_map/reduce_scatter | solution.py:85
  199.4 1.8 copy-start.6
  199.5 1.8 copy-start.3
  199.5 1.7 copy-start.4
  203.0 3.0 copy-start.5
  205.1 0.9 copy-start.1
  207.5 156.3 %all-gather.3.cloned.1.call-start = ((), (), s32[]{:S(2)}) async-start(), calls=%async_computation.6 | async-start | bytes 15925248 | tf_op jit(solution)/shard_map/all_gather | solution.py:74
  210.7 0.9 copy-start.7
  210.7 0.9 copy-start.8
Sparse Core Ops, SparseCore 0:
  30.8 32.5 reduce-scatter.2
  92.1 39.4 all-reduce.3
  138.0 56.5 all-reduce.5
  207.6 24.4 reduce-scatter.4
  234.1 129.5 all-gather.2
